TPU v7x, 32 devices: a whole 2x2x4 slice. The times are simulated.
32 devices in a mesh: row: 8 (over z, x), col: 4 (over y, core).
Axes of the slice: x: 2, y: 2, z: 4, core: 2. Of those that a mesh axis runs over, the one named last changes fastest.
Arguments:
- matrix: float32 [5, 8, 10, 4, 128, 128], P(None, 'row', None, 'col'), may hold values from 0 to 2.5, as said below
- flags: int32 [5, 8, 10, 4], P(None, 'row', None, 'col'), may hold values from 0 to 1, as said below
Outputs:
- factor: float32 [5, 8, 10, 4, 128, 128], P(None, 'row', None, 'col')
Inputs may be any that keep to these rules, and one draw needn't show every extreme that they name: `matrix`: symmetric positive definite, of order 40*128, diagonal at least 1.5. `flags`: 0 marks a float32 tile, 1 a bfloat16 tile; every diagonal tile is 0.
All inputs are finite; a program needn't handle non-finite values.
Results may differ from a plain program's by a relative error of at most 0.0005.
The roundings to bfloat16 on the way count: a program that leaves them out, or rounds other values in their place, can miss the bound.
Values sent between devices are 32-bit elements; how exact they have to be, the bound alone decides.
No kernel may reach another device: no remote copies, remote signals or barrier semaphores. Data moves between devices by JAX's collectives and lax.ppermute only.
A program may use at most 128 MiB of HBM per device.

v0:
```python
import jax
import jax.numpy as jnp
from jax import lax
from jax.sharding import PartitionSpec as P

PT = 4


def spread(value, axis, source):
    kept = jnp.where(lax.axis_index(axis) == source, value, 0).astype(value.dtype)
    return lax.psum(kept, axis)


def storage_round(values):
    narrow = lax.optimization_barrier(values.astype(jnp.bfloat16))
    return narrow.astype(jnp.float32)


def solve_rows(lower_block, rows):
    width = rows.shape[2]
    flat = rows.reshape(-1, width)
    solved = jax.scipy.linalg.solve_triangular(lower_block, flat.T, lower=True).T
    return solved.reshape(rows.shape)


def with_block(solved, lower_block, global_ids, start):
    offset = jnp.clip(global_ids - start, 0, PT - 1)
    block_rows = lower_block.reshape(PT, solved.shape[1], solved.shape[2])[offset]
    inside = (global_ids >= start) & (global_ids < start + PT)
    return jnp.where(inside[:, None, None], block_rows, solved)


def factor_panel(work, start, row_ids, row_count, col_count):
    pieces = []
    for column in range(start, start + PT):
        pieces.append(spread(work[:, column // col_count], "col", column % col_count))
    panel_rows = jnp.concatenate(pieces, axis=2)
    blocks = []
    for tile_row in range(start, start + PT):
        blocks.append(spread(panel_rows[tile_row // row_count], "row", tile_row % row_count))
    dense = jnp.concatenate(blocks, axis=0)
    sym = jnp.tril(dense) + jnp.tril(dense, -1).T
    lower_block = jnp.linalg.cholesky(sym)
    solved = with_block(solve_rows(lower_block, panel_rows), lower_block, row_ids, start)
    return (panel_rows, lower_block, solved)


def apply_update(work, marks, left, right, row_ids, col_ids, low, high):
    exact = jnp.einsum("aik,cjk->acij", left, right, precision=lax.Precision.HIGHEST)
    coarse = jnp.einsum(
        "aik,cjk->acij",
        left.astype(jnp.bfloat16),
        right.astype(jnp.bfloat16),
        preferred_element_type=jnp.float32,
    )
    live = (
        (row_ids[:, None] >= col_ids[None, :])
        & (col_ids >= low)[None, :]
        & (col_ids < high)[None, :]
    )
    updated = jnp.where((marks == 1)[:, :, None, None], work - coarse, work - exact)
    return jnp.where(live[:, :, None, None], updated, work)


def store_panel(work, solved, start, row_ids, col_index, col_count):
    tile = work.shape[2]
    for column in range(start, start + PT):
        slot = column // col_count
        offset = column - start
        piece = solved[:, :, offset * tile : (offset + 1) * tile]
        keep = (row_ids >= start)[:, None, None] & (col_index == column % col_count)
        work = work.at[:, slot].set(jnp.where(keep, piece, work[:, slot]))
    return work


def on_device(matrix, flags):
    row_count = lax.axis_size("row")
    col_count = lax.axis_size("col")
    row_index = lax.axis_index("row")
    col_index = lax.axis_index("col")
    tile_rows = matrix.shape[0]
    tile_cols = matrix.shape[2]
    tile = matrix.shape[4]
    tiles = matrix.reshape(tile_rows, tile_cols, tile, tile)
    marks = flags.reshape(tile_rows, tile_cols)
    row_ids = jnp.arange(tile_rows, dtype=jnp.int32) * row_count + row_index
    col_ids = jnp.arange(tile_cols, dtype=jnp.int32) * col_count + col_index
    work = jnp.where((marks == 1)[:, :, None, None], storage_round(tiles), tiles)
    beyond = 1 << 30
    lefts = []
    rights = []
    for step in range(2):
        start = step * PT
        panel_rows, lower_block, solved = factor_panel(work, start, row_ids, row_count, col_count)
        received = []
        for slot in range(tile_cols):
            column = col_ids[slot]
            piece = lax.dynamic_index_in_dim(solved, column // row_count, 0, keepdims=False)
            received.append(spread(piece, "row", column % row_count))
        right = jnp.stack(received, axis=0)
        lefts.append(solved)
        rights.append(right)
        work = apply_update(work, marks, solved, right, row_ids, col_ids, start + PT, beyond)
        work = store_panel(work, solved, start, row_ids, col_index, col_count)
    final = jnp.where((marks == 1)[:, :, None, None], storage_round(work), work)
    upper = row_ids[:, None] < col_ids[None, :]
    final = jnp.where(upper[:, :, None, None], jnp.float32(0.0), final)
    return final.reshape(matrix.shape)


def solution(mesh):
    return jax.shard_map(
        on_device,
        mesh=mesh,
        in_specs=(P(None, "row", None, "col", None, None), P(None, "row", None, "col")),
        out_specs=P(None, "row", None, "col", None, None),
        check_vma=False,
    )
```

profile of v0, /device:TPU:0, one launch (start us, length us, event | category | flops | bytes accessed | tf_op | source)
XLA Modules:
  0.0 841.9 jit_solution(16314671458284499943)
XLA Ops:
  13.0 42.1 %all-reduce.24.cloned.1.call-done = (f32[5,128,128]{2,1,0:T(8,128)}, f32[5,128,128]{2,1,0:T(8,128)}, f32[5,128,128]{2,1,0:T(8,128)}, f32[5,128,128]{2,1,0:T(8,128)}) async-done(((f32[5,128,128]{2,1,0:T(8,128)}, f32[5,128,128]{2,1,0:T(8,128)}, f32[5,128,128]{2,1,0:T(8,128)}, f32[5,128,128]{2,1,0:T(8,128)}), (f32[5,128,128]{2,1,0:T(8,128)}, f32[5,128,128]{2,1,0:T(8,128)}, f32[5,128,128]{2,1,0:T(8,128)}, ...) | async-done | bytes 1310736 | tf_op jit(solution)/shard_map/psum | solution.py:11
  87.3 52.5 %all-reduce.20.cloned.1.call-done = (f32[128,512]{1,0:T(8,128)}, f32[128,512]{1,0:T(8,128)}, f32[128,512]{1,0:T(8,128)}, f32[128,512]{1,0:T(8,128)}) async-done(((f32[128,512]{1,0:T(8,128)}, f32[128,512]{1,0:T(8,128)}, f32[128,512]{1,0:T(8,128)}, f32[128,512]{1,0:T(8,128)}), (f32[128,512]{1,0:T(8,128)}, f32[128,512]{1,0:T(8,128)}, f32[128,512]{1,0:T(8,128)}, ...) | async-done | bytes 1048592 | tf_op jit(solution)/shard_map/psum | solution.py:11
  144.8 11.7 %cholesky.286 = f32[128,128]{1,0:T(8,128)S(1)} custom-call(f32[128,128]{1,0:T(8,128)S(1)} %cholesky.426), custom_call_target="Cholesky" | custom-call | tf_op jit(solution)/shard_map/jit(cholesky)/cholesky | solution.py:43
  156.7 9.8 %custom-call.27 = f32[1,128,128]{1,2,0:T(8,128)S(1)} custom-call(f32[1,128,128]{2,1,0:T(8,128)S(1)} %get-tuple-element.236), custom_call_target="InvertDiagBlocksLowerTriangular" | custom-call | tf_op jit(solution)/shard_map/jit(cholesky)/cholesky | solution.py:43
  167.2 11.7 %cholesky.305 = f32[128,128]{1,0:T(8,128)S(1)} custom-call(f32[128,128]{1,0:T(8,128)S(1)} %cholesky.430), custom_call_target="Cholesky" | custom-call | tf_op jit(solution)/shard_map/jit(cholesky)/cholesky | solution.py:43
  179.0 9.9 %custom-call.28 = f32[1,128,128]{1,2,0:T(8,128)S(1)} custom-call(f32[1,128,128]{2,1,0:T(8,128)S(1)} %get-tuple-element.233), custom_call_target="InvertDiagBlocksLowerTriangular" | custom-call | tf_op jit(solution)/shard_map/jit(cholesky)/cholesky | solution.py:43
  189.5 11.7 %cholesky.326 = f32[128,128]{1,0:T(8,128)S(1)} custom-call(f32[128,128]{1,0:T(8,128)S(1)} %cholesky.435), custom_call_target="Cholesky" | custom-call | tf_op jit(solution)/shard_map/jit(cholesky)/cholesky | solution.py:43
  202.0 9.8 %custom-call.29 = f32[1,128,128]{1,2,0:T(8,128)S(1)} custom-call(f32[1,128,128]{2,1,0:T(8,128)S(1)} %get-tuple-element.230), custom_call_target="InvertDiagBlocksLowerTriangular" | custom-call | tf_op jit(solution)/shard_map/jit(cholesky)/cholesky | solution.py:43
  212.4 11.9 %cholesky.343 = f32[128,128]{1,0:T(8,128)S(1)} custom-call(f32[128,128]{1,0:T(8,128)S(1)} %convolution_subtract_fusion.11), custom_call_target="Cholesky" | custom-call | tf_op jit(solution)/shard_map/jit(cholesky)/cholesky | solution.py:43
  228.6 8.1 while.12
  236.7 39.3 %custom-call.30 = f32[4,128,128]{1,2,0:T(8,128)S(1)} custom-call(f32[4,128,128]{2,1,0:T(8,128)S(1)} %get-tuple-element.117), custom_call_target="InvertDiagBlocksLowerTriangular" | custom-call | tf_op jit(solution)/shard_map/jit(_solve_triangular)/triangular_solve | solution.py:22
  294.8 115.8 %all-reduce.18.cloned.1.call-done = (f32[1,128,512]{2,1,0:T(8,128)}, f32[1,128,512]{2,1,0:T(8,128)}, f32[1,128,512]{2,1,0:T(8,128)}, f32[1,128,512]{2,1,0:T(8,12...) async-done(((f32[1,128,512]{2,1,0:T(8,128)}, ...) | async-done | bytes 2621456 | tf_op jit(solution)/shard_map/psum | solution.py:11
  425.9 38.2 %all-reduce.22.cloned.1.call-done = (f32[5,128,128]{2,1,0:T(8,128)}, f32[5,128,128]{2,1,0:T(8,128)}, f32[5,128,128]{2,1,0:T(8,128)}, f32[5,128,128]{2,1,0:T(8,128)}) async-done(((f32[5,128,128]{2,1,0:T(8,128)}, f32[5,128,128]{2,1,0:T(8,128)}, f32[5,128,128]{2,1,0:T(8,128)}, f32[5,128,128]{2,1,0:T(8,128)}), (f32[5,128,128]{2,1,0:T(8,128)}, f32[5,128,128]{2,1,0:T(8,128)}, f32[5,128,128]{2,1,0:T(8,128)}, ...) | async-done | bytes 1310736 | tf_op jit(solution)/shard_map/psum | solution.py:11
  471.0 77.9 %all-reduce.16.cloned.1.call-done = (f32[128,512]{1,0:T(8,128)}, f32[128,512]{1,0:T(8,128)}, f32[128,512]{1,0:T(8,128)}, f32[128,512]{1,0:T(8,128)}) async-done(((f32[128,512]{1,0:T(8,128)}, f32[128,512]{1,0:T(8,128)}, f32[128,512]{1,0:T(8,128)}, f32[128,512]{1,0:T(8,128)}), (f32[128,512]{1,0:T(8,128)}, f32[128,512]{1,0:T(8,128)}, f32[128,512]{1,0:T(8,128)}, ...) | async-done | bytes 1048592 | tf_op jit(solution)/shard_map/psum | solution.py:11
  554.0 11.7 %cholesky.358 = f32[128,128]{1,0:T(8,128)S(1)} custom-call(f32[128,128]{1,0:T(8,128)S(1)} %cholesky.439), custom_call_target="Cholesky" | custom-call | tf_op jit(solution)/shard_map/jit(cholesky)/cholesky | solution.py:43
  565.9 9.8 %custom-call.31 = f32[1,128,128]{1,2,0:T(8,128)S(1)} custom-call(f32[1,128,128]{2,1,0:T(8,128)S(1)} %get-tuple-element.226), custom_call_target="InvertDiagBlocksLowerTriangular" | custom-call | tf_op jit(solution)/shard_map/jit(cholesky)/cholesky | solution.py:43
  576.4 11.7 %cholesky.377 = f32[128,128]{1,0:T(8,128)S(1)} custom-call(f32[128,128]{1,0:T(8,128)S(1)} %cholesky.443), custom_call_target="Cholesky" | custom-call | tf_op jit(solution)/shard_map/jit(cholesky)/cholesky | solution.py:43
  589.8 9.8 %custom-call.32 = f32[1,128,128]{1,2,0:T(8,128)S(1)} custom-call(f32[1,128,128]{2,1,0:T(8,128)S(1)} %get-tuple-element.223), custom_call_target="InvertDiagBlocksLowerTriangular" | custom-call | tf_op jit(solution)/shard_map/jit(cholesky)/cholesky | solution.py:43
  600.3 11.7 %cholesky.398 = f32[128,128]{1,0:T(8,128)S(1)} custom-call(f32[128,128]{1,0:T(8,128)S(1)} %cholesky.448), custom_call_target="Cholesky" | custom-call | tf_op jit(solution)/shard_map/jit(cholesky)/cholesky | solution.py:43
  612.7 9.8 %custom-call.33 = f32[1,128,128]{1,2,0:T(8,128)S(1)} custom-call(f32[1,128,128]{2,1,0:T(8,128)S(1)} %get-tuple-element.220), custom_call_target="InvertDiagBlocksLowerTriangular" | custom-call | tf_op jit(solution)/shard_map/jit(cholesky)/cholesky | solution.py:43
  623.1 11.9 %cholesky.415 = f32[128,128]{1,0:T(8,128)S(1)} custom-call(f32[128,128]{1,0:T(8,128)S(1)} %convolution_subtract_fusion.10), custom_call_target="Cholesky" | custom-call | tf_op jit(solution)/shard_map/jit(cholesky)/cholesky | solution.py:43
  638.4 7.3 while.13
  645.7 39.3 %custom-call.34 = f32[4,128,128]{1,2,0:T(8,128)S(1)} custom-call(f32[4,128,128]{2,1,0:T(8,128)S(1)} %get-tuple-element.118), custom_call_target="InvertDiagBlocksLowerTriangular" | custom-call | tf_op jit(solution)/shard_map/jit(_solve_triangular)/triangular_solve | solution.py:22
  703.2 116.4 %all-reduce.14.cloned.1.call-done = (f32[1,128,512]{2,1,0:T(8,128)}, f32[1,128,512]{2,1,0:T(8,128)}, f32[1,128,512]{2,1,0:T(8,128)}, f32[1,128,512]{2,1,0:T(8,12...) async-done(((f32[1,128,512]{2,1,0:T(8,128)}, ...) | async-done | bytes 2621456 | tf_op jit(solution)/shard_map/psum | solution.py:11
  (226 shorter events, 122.3 us)
Async XLA Ops:
  6.5 3.2 copy-start.4
  6.5 48.5 %all-reduce.24.cloned.1.call-start = ((), (), s32[]{:S(2)}) async-start(), calls=%async_computation.5 | async-start | bytes 2621440 | tf_op jit(solution)/shard_map/psum | solution.py:11
  10.1 1.7 copy-start.2
  12.9 126.9 %all-reduce.20.cloned.1.call-start = ((), (), s32[]{:S(2)}) async-start(), calls=%async_computation.3 | async-start | bytes 2097152 | tf_op jit(solution)/shard_map/psum | solution.py:11
  59.1 1.1 copy-start.5
  61.3 349.3 %all-reduce.18.cloned.1.call-start = ((), (), s32[]{:S(2)}) async-start(), calls=%async_computation.2 | async-start | bytes 5242880 | tf_op jit(solution)/shard_map/psum | solution.py:11
  294.1 169.9 %all-reduce.22.cloned.1.call-start = ((), (), s32[]{:S(2)}) async-start(), calls=%async_computation.4 | async-start | bytes 2621440 | tf_op jit(solution)/shard_map/psum | solution.py:11
  410.6 5.0 copy-start.11
  410.6 5.0 copy-start.10
  410.6 5.1 copy-start.9
  410.6 5.1 copy-start.8
  410.6 5.1 copy-start.7
  415.8 5.4 copy-start.3
  423.0 1.7 copy-start
  425.8 123.0 %all-reduce.16.cloned.1.call-start = ((), (), s32[]{:S(2)}) async-start(), calls=%async_computation.1 | async-start | bytes 2097152 | tf_op jit(solution)/shard_map/psum | solution.py:11
  468.1 1.1 copy-start.6
  470.2 349.3 %all-reduce.14.cloned.1.call-start = ((), (), s32[]{:S(2)}) async-start(), calls=%async_computation | async-start | bytes 5242880 | tf_op jit(solution)/shard_map/psum | solution.py:11
  819.6 5.0 copy-start.16
  819.6 5.0 copy-start.15
  819.6 5.1 copy-start.14
  819.6 5.1 copy-start.13
  819.6 5.1 copy-start.12
  824.7 5.6 copy-start.1
Sparse Core Ops, SparseCore 0:
  13.0 41.9 all-reduce.23
  61.4 78.4 all-reduce.19
  294.3 116.2 all-reduce.17
  425.9 38.0 all-reduce.21
  470.4 78.4 all-reduce.15
  703.2 116.2 all-reduce.13
where the time goes:
time: 853 us; the launch traced here: 842 us
  waiting for transfers between devices  443 us (52%)
  other arithmetic  256 us (30%)
  local copies, waits for them, and re-layouts  60.7 us (7%)
  between operations  45 us (5%)
  matrix products  36.4 us (4%)
    psum x6, waiting for transfers between devices, spread(): return lax.psum(kept, axis)  443 us
    another operation x29, other arithmetic, factor_panel(): lower_block = jnp.linalg.cholesky(sym)  158 us
    another operation x5, other arithmetic, solve_rows(): jax.scipy.linalg.solve_triangular(lower_block, flat.T, lower=True)  79.2 us
    unnamed x65, local copies, waits for them, and re-layouts  29.8 us
    another operation x14, matrix products, solve_rows(): jax.scipy.linalg.solve_triangular(lower_block, flat.T, lower=True)  19.1 us
  transfers between devices with their start and end apart: 6, of which 6 were waited for; matrix products, arithmetic and copies ran while one was open for 0% of the time, Pallas kernels for 0%

commit v1 on v0

--- a/solution.py
+++ b/solution.py
@@ -8,7 +8,7 @@
 
 def spread(value, axis, source):
     kept = jnp.where(lax.axis_index(axis) == source, value, 0).astype(value.dtype)
-    return lax.psum(kept, axis)
+    return jnp.sum(jax.lax.all_gather(kept, axis), axis=0)
 
 
 def storage_round(values):

time: 853 us -> 1940 us (2.27)
  waiting for transfers between devices: 443 us -> 1410 us
  other arithmetic: 256 us -> 316 us
  local copies, waits for them, and re-layouts: 60.7 us -> 111 us
    all_gather x0 -> x36, waiting for transfers between devices: none -> 1410 us  [spread(): return jnp.sum(jax.lax.all_gather(kept, axis), axis=0)]
    psum x6 -> x0, waiting for transfers between devices: 443 us -> none  [spread(): return lax.psum(kept, axis)]
    reduce_sum x0 -> x36, other arithmetic: none -> 63.7 us  [spread(): return jnp.sum(jax.lax.all_gather(kept, axis), axis=0)]
    select_n x0 -> x36, local copies, waits for them, and re-layouts: none -> 32.8 us  [spread(): jnp.where(lax.axis_index(axis) == source, value, 0).astype(value.dtype)]
  transfers between devices with their start and end apart: 6 -> 36, of which waited for: 6 -> 36; matrix products, arithmetic and copies ran while one was open for 0% -> 5% of each run, Pallas kernels for 0% -> 0%
where the time goes in v1:
time: 1940 us; the launch traced here: 1930 us
  waiting for transfers between devices  1410 us (73%)
  other arithmetic  316 us (16%)
  local copies, waits for them, and re-layouts  111 us (6%)
  matrix products  46.7 us (2%)
  between operations  45.7 us (2%)
    all_gather x36, waiting for transfers between devices, spread(): return jnp.sum(jax.lax.all_gather(kept, axis), axis=0)  1410 us
    another operation x29, other arithmetic, factor_panel(): lower_block = jnp.linalg.cholesky(sym)  158 us
    another operation x5, other arithmetic, solve_rows(): jax.scipy.linalg.solve_triangular(lower_block, flat.T, lower=True)  81.1 us
    reduce_sum x36, other arithmetic, spread(): return jnp.sum(jax.lax.all_gather(kept, axis), axis=0)  63.7 us
  transfers between devices with their start and end apart: 36, of which 36 were waited for; matrix products, arithmetic and copies ran while one was open for 5% of the time, Pallas kernels for 0%

profile of v1, /device:TPU:0, one launch (start us, length us, event | category | flops | bytes accessed | tf_op | source)
XLA Modules:
  0.0 1932.0 jit_solution(10071410157549695500)
XLA Ops:
  148.4 47.7 %all-gather.47.cloned.1.call-done = f32[8,128,512]{2,1,0:T(8,128)} async-done(((f32[1,128,512]{2,1,0:T(8,128)}), f32[8,128,512]{2,1,0:T(8,128)}) %all-gather.47.cloned.1.call-update) | async-done | bytes 2097168 | tf_op jit(solution)/shard_map/all_gather | solution.py:11
  198.0 47.8 %all-gather.49.cloned.1.call-done = f32[8,128,512]{2,1,0:T(8,128)} async-done(((f32[1,128,512]{2,1,0:T(8,128)}), f32[8,128,512]{2,1,0:T(8,128)}) %all-gather.49.cloned.1.call-update) | async-done | bytes 2097168 | tf_op jit(solution)/shard_map/all_gather | solution.py:11
  247.8 47.8 %all-gather.51.cloned.1.call-done = f32[8,128,512]{2,1,0:T(8,128)} async-done(((f32[1,128,512]{2,1,0:T(8,128)}), f32[8,128,512]{2,1,0:T(8,128)}) %all-gather.51.cloned.1.call-update) | async-done | bytes 2097168 | tf_op jit(solution)/shard_map/all_gather | solution.py:11
  509.1 47.8 %all-gather.53.cloned.1.call-done = f32[8,128,512]{2,1,0:T(8,128)} async-done(((f32[1,128,512]{2,1,0:T(8,128)}), f32[8,128,512]{2,1,0:T(8,128)}) %all-gather.53.cloned.1.call-update) | async-done | bytes 2097168 | tf_op jit(solution)/shard_map/all_gather | solution.py:11
  558.7 48.0 %all-gather.57.cloned.1.call-done = f32[8,128,512]{2,1,0:T(8,128)} async-done(((f32[1,128,512]{2,1,0:T(8,128)}), f32[8,128,512]{2,1,0:T(8,128)}) %all-gather.57.cloned.1.call-update) | async-done | bytes 2097168 | tf_op jit(solution)/shard_map/all_gather | solution.py:11
  608.5 47.8 %all-gather.59.cloned.1.call-done = f32[8,128,512]{2,1,0:T(8,128)} async-done(((f32[1,128,512]{2,1,0:T(8,128)}), f32[8,128,512]{2,1,0:T(8,128)}) %all-gather.59.cloned.1.call-update) | async-done | bytes 2097168 | tf_op jit(solution)/shard_map/all_gather | solution.py:11
  658.1 48.0 %all-gather.61.cloned.1.call-done = f32[8,128,512]{2,1,0:T(8,128)} async-done(((f32[1,128,512]{2,1,0:T(8,128)}), f32[8,128,512]{2,1,0:T(8,128)}) %all-gather.61.cloned.1.call-update) | async-done | bytes 2097168 | tf_op jit(solution)/shard_map/all_gather | solution.py:11
  707.9 47.8 %all-gather.63.cloned.1.call-done = f32[8,128,512]{2,1,0:T(8,128)} async-done(((f32[1,128,512]{2,1,0:T(8,128)}), f32[8,128,512]{2,1,0:T(8,128)}) %all-gather.63.cloned.1.call-update) | async-done | bytes 2097168 | tf_op jit(solution)/shard_map/all_gather | solution.py:11
  757.5 47.8 %all-gather.65.cloned.1.call-done = f32[8,128,512]{2,1,0:T(8,128)} async-done(((f32[1,128,512]{2,1,0:T(8,128)}), f32[8,128,512]{2,1,0:T(8,128)}) %all-gather.65.cloned.1.call-update) | async-done | bytes 2097168 | tf_op jit(solution)/shard_map/all_gather | solution.py:11
  807.2 47.8 %all-gather.67.cloned.1.call-done = f32[8,128,512]{2,1,0:T(8,128)} async-done(((f32[1,128,512]{2,1,0:T(8,128)}), f32[8,128,512]{2,1,0:T(8,128)}) %all-gather.67.cloned.1.call-update) | async-done | bytes 2097168 | tf_op jit(solution)/shard_map/all_gather | solution.py:11
  856.8 47.8 %all-gather.69.cloned.1.call-done = f32[8,128,512]{2,1,0:T(8,128)} async-done(((f32[1,128,512]{2,1,0:T(8,128)}), f32[8,128,512]{2,1,0:T(8,128)}) %all-gather.69.cloned.1.call-update) | async-done | bytes 2097168 | tf_op jit(solution)/shard_map/all_gather | solution.py:11
  913.6 40.6 %all-gather.71.cloned.1.call-done = f32[8,128,512]{2,1,0:T(8,128)} async-done(((f32[1,128,512]{2,1,0:T(8,128)}), f32[8,128,512]{2,1,0:T(8,128)}) %all-gather.71.cloned.1.call-update) | async-done | bytes 2097168 | tf_op jit(solution)/shard_map/all_gather | solution.py:11
  1057.7 41.5 %all-gather.73.cloned.1.call-done = f32[8,128,512]{2,1,0:T(8,128)} async-done(((f32[1,128,512]{2,1,0:T(8,128)}), f32[8,128,512]{2,1,0:T(8,128)}) %all-gather.73.cloned.1.call-update) | async-done | bytes 2097168 | tf_op jit(solution)/shard_map/all_gather | solution.py:11
  1101.0 47.8 %all-gather.75.cloned.1.call-done = f32[8,128,512]{2,1,0:T(8,128)} async-done(((f32[1,128,512]{2,1,0:T(8,128)}), f32[8,128,512]{2,1,0:T(8,128)}) %all-gather.75.cloned.1.call-update) | async-done | bytes 2097168 | tf_op jit(solution)/shard_map/all_gather | solution.py:11
  1150.7 47.9 %all-gather.77.cloned.1.call-done = f32[8,128,512]{2,1,0:T(8,128)} async-done(((f32[1,128,512]{2,1,0:T(8,128)}), f32[8,128,512]{2,1,0:T(8,128)}) %all-gather.77.cloned.1.call-update) | async-done | bytes 2097168 | tf_op jit(solution)/shard_map/all_gather | solution.py:11
  1200.4 47.8 %all-gather.79.cloned.1.call-done = f32[8,128,512]{2,1,0:T(8,128)} async-done(((f32[1,128,512]{2,1,0:T(8,128)}), f32[8,128,512]{2,1,0:T(8,128)}) %all-gather.79.cloned.1.call-update) | async-done | bytes 2097168 | tf_op jit(solution)/shard_map/all_gather | solution.py:11
  1461.3 48.0 %all-gather.81.cloned.1.call-done = f32[8,128,512]{2,1,0:T(8,128)} async-done(((f32[1,128,512]{2,1,0:T(8,128)}), f32[8,128,512]{2,1,0:T(8,128)}) %all-gather.81.cloned.1.call-update) | async-done | bytes 2097168 | tf_op jit(solution)/shard_map/all_gather | solution.py:11
  1511.1 48.0 %all-gather.85.cloned.1.call-done = f32[8,128,512]{2,1,0:T(8,128)} async-done(((f32[1,128,512]{2,1,0:T(8,128)}), f32[8,128,512]{2,1,0:T(8,128)}) %all-gather.85.cloned.1.call-update) | async-done | bytes 2097168 | tf_op jit(solution)/shard_map/all_gather | solution.py:11
  1560.9 47.8 %all-gather.87.cloned.1.call-done = f32[8,128,512]{2,1,0:T(8,128)} async-done(((f32[1,128,512]{2,1,0:T(8,128)}), f32[8,128,512]{2,1,0:T(8,128)}) %all-gather.87.cloned.1.call-update) | async-done | bytes 2097168 | tf_op jit(solution)/shard_map/all_gather | solution.py:11
  1610.5 48.0 %all-gather.89.cloned.1.call-done = f32[8,128,512]{2,1,0:T(8,128)} async-done(((f32[1,128,512]{2,1,0:T(8,128)}), f32[8,128,512]{2,1,0:T(8,128)}) %all-gather.89.cloned.1.call-update) | async-done | bytes 2097168 | tf_op jit(solution)/shard_map/all_gather | solution.py:11
  1660.3 48.0 %all-gather.91.cloned.1.call-done = f32[8,128,512]{2,1,0:T(8,128)} async-done(((f32[1,128,512]{2,1,0:T(8,128)}), f32[8,128,512]{2,1,0:T(8,128)}) %all-gather.91.cloned.1.call-update) | async-done | bytes 2097168 | tf_op jit(solution)/shard_map/all_gather | solution.py:11
  1710.0 47.8 %all-gather.93.cloned.1.call-done = f32[8,128,512]{2,1,0:T(8,128)} async-done(((f32[1,128,512]{2,1,0:T(8,128)}), f32[8,128,512]{2,1,0:T(8,128)}) %all-gather.93.cloned.1.call-update) | async-done | bytes 2097168 | tf_op jit(solution)/shard_map/all_gather | solution.py:11
  1759.7 48.0 %all-gather.95.cloned.1.call-done = f32[8,128,512]{2,1,0:T(8,128)} async-done(((f32[1,128,512]{2,1,0:T(8,128)}), f32[8,128,512]{2,1,0:T(8,128)}) %all-gather.95.cloned.1.call-update) | async-done | bytes 2097168 | tf_op jit(solution)/shard_map/all_gather | solution.py:11
  1809.5 48.0 %all-gather.97.cloned.1.call-done = f32[8,128,512]{2,1,0:T(8,128)} async-done(((f32[1,128,512]{2,1,0:T(8,128)}), f32[8,128,512]{2,1,0:T(8,128)}) %all-gather.97.cloned.1.call-update) | async-done | bytes 2097168 | tf_op jit(solution)/shard_map/all_gather | solution.py:11
  (397 shorter events, 774.6 us)
Async XLA Ops:
  17.2 129.2 %all-gather.45.cloned.1.call-start = ((), (), s32[]{:S(2)}) async-start(), calls=%async_computation | async-start | bytes 2359296 | tf_op jit(solution)/shard_map/all_gather | solution.py:11
  98.0 147.8 %all-gather.49.cloned.1.call-start = ((), (), s32[]{:S(2)}) async-start(), calls=%async_computation.2 | async-start | bytes 2359296 | tf_op jit(solution)/shard_map/all_gather | solution.py:11
  99.0 196.6 %all-gather.51.cloned.1.call-start = ((), (), s32[]{:S(2)}) async-start(), calls=%async_computation.3 | async-start | bytes 2359296 | tf_op jit(solution)/shard_map/all_gather | solution.py:11
  99.9 407.4 %all-gather.55.cloned.1.call-start = ((), (), s32[]{:S(2)}) async-start(), calls=%async_computation.5 | async-start | bytes 2359296 | tf_op jit(solution)/shard_map/all_gather | solution.py:11
  463.0 143.7 %all-gather.57.cloned.1.call-start = ((), (), s32[]{:S(2)}) async-start(), calls=%async_computation.6 | async-start | bytes 2359296 | tf_op jit(solution)/shard_map/all_gather | solution.py:11
  464.9 191.4 %all-gather.59.cloned.1.call-start = ((), (), s32[]{:S(2)}) async-start(), calls=%async_computation.7 | async-start | bytes 2359296 | tf_op jit(solution)/shard_map/all_gather | solution.py:11
  465.8 240.3 %all-gather.61.cloned.1.call-start = ((), (), s32[]{:S(2)}) async-start(), calls=%async_computation.8 | async-start | bytes 2359296 | tf_op jit(solution)/shard_map/all_gather | solution.py:11
  466.7 289.0 %all-gather.63.cloned.1.call-start = ((), (), s32[]{:S(2)}) async-start(), calls=%async_computation.9 | async-start | bytes 2359296 | tf_op jit(solution)/shard_map/all_gather | solution.py:11
  467.7 337.7 %all-gather.65.cloned.1.call-start = ((), (), s32[]{:S(2)}) async-start(), calls=%async_computation.10 | async-start | bytes 2359296 | tf_op jit(solution)/shard_map/all_gather | solution.py:11
  468.6 386.4 %all-gather.67.cloned.1.call-start = ((), (), s32[]{:S(2)}) async-start(), calls=%async_computation.11 | async-start | bytes 2359296 | tf_op jit(solution)/shard_map/all_gather | solution.py:11
  469.5 435.1 %all-gather.69.cloned.1.call-start = ((), (), s32[]{:S(2)}) async-start(), calls=%async_computation.12 | async-start | bytes 2359296 | tf_op jit(solution)/shard_map/all_gather | solution.py:11
  470.4 483.8 %all-gather.71.cloned.1.call-start = ((), (), s32[]{:S(2)}) async-start(), calls=%async_computation.13 | async-start | bytes 2359296 | tf_op jit(solution)/shard_map/all_gather | solution.py:11
  471.5 516.7 %all-gather.109.cloned.1.call-start = ((), (), s32[]{:S(2)}) async-start(), calls=%async_computation.32 | async-start | bytes 1638400 | tf_op jit(solution)/shard_map/all_gather | solution.py:11
  1050.9 147.7 %all-gather.77.cloned.1.call-start = ((), (), s32[]{:S(2)}) async-start(), calls=%async_computation.16 | async-start | bytes 2359296 | tf_op jit(solution)/shard_map/all_gather | solution.py:11
  1051.8 196.4 %all-gather.79.cloned.1.call-start = ((), (), s32[]{:S(2)}) async-start(), calls=%async_computation.17 | async-start | bytes 2359296 | tf_op jit(solution)/shard_map/all_gather | solution.py:11
  1052.7 406.7 %all-gather.83.cloned.1.call-start = ((), (), s32[]{:S(2)}) async-start(), calls=%async_computation.19 | async-start | bytes 2359296 | tf_op jit(solution)/shard_map/all_gather | solution.py:11
  1412.7 146.4 %all-gather.85.cloned.1.call-start = ((), (), s32[]{:S(2)}) async-start(), calls=%async_computation.20 | async-start | bytes 2359296 | tf_op jit(solution)/shard_map/all_gather | solution.py:11
  1414.5 194.1 %all-gather.87.cloned.1.call-start = ((), (), s32[]{:S(2)}) async-start(), calls=%async_computation.21 | async-start | bytes 2359296 | tf_op jit(solution)/shard_map/all_gather | solution.py:11
  1415.5 243.0 %all-gather.89.cloned.1.call-start = ((), (), s32[]{:S(2)}) async-start(), calls=%async_computation.22 | async-start | bytes 2359296 | tf_op jit(solution)/shard_map/all_gather | solution.py:11
  1416.4 291.8 %all-gather.91.cloned.1.call-start = ((), (), s32[]{:S(2)}) async-start(), calls=%async_computation.23 | async-start | bytes 2359296 | tf_op jit(solution)/shard_map/all_gather | solution.py:11
  1417.3 340.5 %all-gather.93.cloned.1.call-start = ((), (), s32[]{:S(2)}) async-start(), calls=%async_computation.24 | async-start | bytes 2359296 | tf_op jit(solution)/shard_map/all_gather | solution.py:11
  1418.2 389.4 %all-gather.95.cloned.1.call-start = ((), (), s32[]{:S(2)}) async-start(), calls=%async_computation.25 | async-start | bytes 2359296 | tf_op jit(solution)/shard_map/all_gather | solution.py:11
  1419.2 438.2 %all-gather.97.cloned.1.call-start = ((), (), s32[]{:S(2)}) async-start(), calls=%async_computation.26 | async-start | bytes 2359296 | tf_op jit(solution)/shard_map/all_gather | solution.py:11
  1420.1 487.0 %all-gather.99.cloned.1.call-start = ((), (), s32[]{:S(2)}) async-start(), calls=%async_computation.27 | async-start | bytes 2359296 | tf_op jit(solution)/shard_map/all_gather | solution.py:11
  (28 other events, 1522.5 us)
Sparse Core Ops, SparseCore 0:
  97.2 49.1 all-gather.44
  148.4 47.6 all-gather.46
  198.2 47.6 all-gather.48
  247.9 47.6 all-gather.50
  509.2 47.6 all-gather.52
  559.0 47.6 all-gather.56
  608.7 47.6 all-gather.58
  658.4 47.6 all-gather.60
  708.1 47.6 all-gather.62
  757.7 47.6 all-gather.64
  807.3 47.6 all-gather.66
  856.9 47.6 all-gather.68
  906.6 47.6 all-gather.70
  1050.1 49.0 all-gather.72
  1101.2 47.6 all-gather.74
  1151.0 47.6 all-gather.76
  1200.6 47.6 all-gather.78
  1461.6 47.6 all-gather.80
  1511.4 47.6 all-gather.84
  1561.0 47.6 all-gather.86
  1610.8 47.6 all-gather.88
  1710.2 47.6 all-gather.92
  1760.0 47.6 all-gather.94
  1859.4 47.6 all-gather.98
  (12 shorter events, 336.3 us)
